TPU v7x, 32 devices: a whole 2x2x4 slice. The times are simulated.
32 devices in a mesh: ka: 8 (over z, core), band: 4 (over y, x).
Axes of the slice: x: 2, y: 2, z: 4, core: 2. Of those that a mesh axis runs over, the one named last changes fastest.
Arguments:
- occ_rows: bfloat16 [8, 2048, 128], P('ka', 'band'), may hold values from -0.5 to 0.5
- vir_rows: bfloat16 [8, 2048, 896], P('ka', 'band'), may hold values from -0.1875 to 0.1875
- trial_vectors: float32 [8, 2, 128, 896], P('ka', None, None, 'band'), may hold values from -6 to 6
- occ_energy: float32 [8, 128], P('ka'), may hold values from -1.2 to -0.3
- vir_energy: float32 [8, 896], P('ka', 'band'), may hold values from 0.1 to 1.5
- coulomb: bfloat16 [2048, 2048], P('band'), may hold values from -0.09375 to 0.09375
- exch_kernel: bfloat16 [8, 2048, 2048], P(None, 'band'), as said below
- minus_table: int32 [8, 8], replicated, may hold values from 0 to 7, as said below
Outputs:
- sigma_vectors: float32 [8, 2, 128, 896], P('ka', None, None, 'band')
Inputs may be any that keep to these rules, and one draw needn't show every extreme that they name: minus_table[k, q] is the k-point k - q on a group of 8 k-points: every row and every column holds each index once, and one q gives minus_table[k, q] == k for every k. Each exch_kernel[q] is symmetric.
All inputs are finite; a program needn't handle non-finite values.
Results may differ from a plain program's by a relative error of at most 0.0051.
Values may be sent and summed in bfloat16 or wider, within the bound.
A program may use at most 128 MiB of HBM per device.

v0:
```python
import jax
import jax.numpy as jnp
from jax import lax
from jax.sharding import PartitionSpec as P


def per_device(
    occ_rows, vir_rows, trial_vectors, occ_energy, vir_energy, coulomb, exch_kernel, minus_table
):
    vectors = trial_vectors.shape[1]
    own_rows = occ_rows.shape[1]
    kpoints = lax.axis_size("ka")
    self_point = lax.axis_index("ka")
    trial_half = trial_vectors[0].astype(jnp.bfloat16)
    trial_full, vir_full = (
        lax.all_gather(trial_half, "band", axis=2, tiled=True),
        lax.all_gather(vir_rows[0], "band", axis=0, tiled=True),
    )
    auxiliary = vir_full.shape[0]
    occ_own = occ_rows[0]
    vir_own = vir_rows[0]
    mixed_rows = jnp.einsum(
        "ri,via->vra", occ_own, trial_full, preferred_element_type=jnp.float32
    ).astype(jnp.bfloat16)
    pair_block = jnp.einsum(
        "vra,na->vrn", mixed_rows, vir_full, preferred_element_type=jnp.float32
    ).astype(jnp.bfloat16)
    density_own = jnp.sum(
        mixed_rows.astype(jnp.float32) * vir_own.astype(jnp.float32)[None], axis=2
    )
    density_sum = lax.psum(density_own, "ka")
    density_half = lax.all_gather(density_sum.astype(jnp.bfloat16), "band", axis=1, tiled=True)
    potential = jnp.einsum("vn,rn->vr", density_half, coulomb, preferred_element_type=jnp.float32)
    piece_width = auxiliary // kpoints
    kernel_cols = lax.dynamic_slice_in_dim(exch_kernel, self_point * piece_width, piece_width, 2)
    split_pairs = pair_block.reshape(vectors, own_rows, kpoints, piece_width)
    moved_pairs = jnp.take(
        lax.all_to_all(split_pairs, "ka", split_axis=2, concat_axis=2, tiled=True),
        minus_table,
        axis=2,
    )
    summed = jnp.einsum(
        "vrkqc,qrc->vrkc", moved_pairs, kernel_cols, preferred_element_type=jnp.float32
    )
    screened = lax.all_to_all(
        summed.astype(jnp.bfloat16), "ka", split_axis=2, concat_axis=2, tiled=True
    )
    screened = screened.reshape(vectors, own_rows, auxiliary)
    product = jnp.einsum("vrn,na->vra", screened, vir_full, preferred_element_type=jnp.float32)
    weights = (2.0 * potential[:, :, None] * vir_own.astype(jnp.float32)[None] - product).astype(
        jnp.bfloat16
    )
    partial_sums = jnp.einsum("ri,vra->via", occ_own, weights, preferred_element_type=jnp.float32)
    coupled = lax.psum_scatter(partial_sums, "band", scatter_dimension=2, tiled=True)
    energy_gaps = vir_energy[0][None, :] - occ_energy[0][:, None]
    return (energy_gaps[None] * trial_vectors[0] + coupled)[None]


def solution(mesh):
    in_specs = (
        P("ka", "band", None),
        P("ka", "band", None),
        P("ka", None, None, "band"),
        P("ka", None),
        P("ka", "band"),
        P("band", None),
        P(None, "band", None),
        P(),
    )
    out_specs = P("ka", None, None, "band")
    return jax.shard_map(
        per_device, mesh=mesh, in_specs=in_specs, out_specs=out_specs, check_vma=False
    )
```

profile of v0, /device:TPU:0, one launch (start us, length us, event | category | flops | bytes accessed | tf_op | source)
XLA Modules:
  0.0 375.4 jit_solution(881767993368550166)
XLA Ops:
  6.5 0.0 copy-start
  6.5 0.0 copy-start.1
  6.5 0.0 all-gather.3.cloned.1.call-start
  6.5 0.7 all-gather.3.cloned.1.call-update
  7.3 0.0 copy-start.2
  7.3 2.6 bitcast_convert_fusion.1
  9.9 2.8 copy.14
  12.7 0.0 copy-done.1
  12.7 13.6 %all_gather.9 = bf16[2,128,896]{1,2,0:T(8,128)(2,1)S(1)} all-gather(bf16[2,128,224]{1,2,0:T(8,128)(2,1)S(1)} %bitcast_convert_fusion.2), channel_id=1, replica_groups=mesh['ka'=8,'band'=4] {'band'}, dimensions={2}, use_global_device_ids=true | all-gather | bytes 573440 | tf_op jit(solution)/shard_map/all_gather | solution.py:16
  26.3 0.0 copy-done.2
  26.3 3.4 multiply_reduce_fusion.1
  29.7 31.7 %all-gather.3.cloned.1.call-done = bf16[1,2048,896]{2,1,0:T(8,128)(2,1)} async-done(((bf16[1,512,896]{2,1,0:T(8,128)(2,1)}), bf16[1,2048,896]{2,1,0:T(8,128)(2,1)}) %all-gather.3.cloned.1.call-update) | async-done | bytes 3670032 | tf_op jit(solution)/shard_map/all_gather | solution.py:17
  61.4 7.1 %convolution_convert_fusion = bf16[2,512,2048]{2,1,0:T(8,128)(2,1)S(1)} fusion(bf16[1,2048,896]{2,1,0:T(8,128)(2,1)} %all-gather.3.cloned.1.call-done, bf16[2,896,512]{2,1,0:T(8,128)(2,1)} %get-tuple-element.6), kind=kOutput, calls=%fused_computation.4 | convolution fusion | flops 3760193536 | bytes 9699328 | tf_op jit(solution)/shard_map/vra,na->vrn/dot_general | solution.py:25
  68.5 2.4 copy.35
  70.9 0.0 copy-start.3
  70.9 4.7 %all-to-all-start = ((bf16[2,512,8,256]{3,1,0,2:T(8,128)(2,1)}), bf16[2,512,8,256]{3,1,0,2:T(8,128)(2,1)}, u32[]{:S(2)}, u32[]{:S(2)}) async-start(bf16[2,512,8,256]{3,1,0,2:T(8,128)(2,1)} %bitcast.58), calls=%async_computation | async-start | bytes 8388608 | tf_op jit(solution)/shard_map/all_to_all | solution.py:38
  75.7 0.0 copy-done.3
  75.7 0.1 reshape.47
  75.8 4.0 %bitcast_convert_fusion = f32[512,256,8]{1,0,2:T(8,128)} fusion(bf16[8,512,2048]{2,1,0:T(8,128)(2,1)} %param.14, s32[]{:T(128)S(6)} %select_n.12), kind=kLoop, calls=%fused_computation.10 | loop fusion | flops 1048576 | bytes 6291460
  79.8 89.9 %all-to-all-done = bf16[2,512,8,256]{3,1,0,2:T(8,128)(2,1)} async-done(((bf16[2,512,8,256]{3,1,0,2:T(8,128)(2,1)}), bf16[2,512,8,256]{3,1,0,2:T(8,128)(2,1)}, u32[]{:S(2)}, u32[]{:S(2)}) %all-to-all-start) | async-done | bytes 4194336 | tf_op jit(solution)/shard_map/all_to_all | solution.py:38
  169.7 4.5 %copy.17 = bf16[2,512,8,256]{3,1,2,0:T(8,128)(2,1)} copy(bf16[2,512,8,256]{3,1,0,2:T(8,128)(2,1)} %all-to-all-done) | data formatting | bytes 8388608 | tf_op jit(solution)/shard_map/all_to_all | solution.py:38
  174.2 14.6 %gather_fusion = bf16[64,2,512,256]{3,2,1,0:T(8,128)(2,1)} fusion(bf16[2,512,8,256]{3,1,2,0:T(8,128)(2,1)} %copy.17, s32[1024]{0:T(1024)S(1)} %pad_clamp_fusion), kind=kCustom, calls=%fused_computation | custom fusion | bytes 67109120 | tf_op jit(solution)/shard_map/jit(_take)/gather | solution.py:37
  188.8 19.3 %multiply_reduce_fusion = bf16[512,256,2,8]{1,0,2,3:T(8,128)(2,1)} fusion(f32[512,256,8]{1,0,2:T(8,128)} %bitcast_convert_fusion, bf16[8,8,2,512,256]{4,3,2,1,0:T(8,128)(2,1)} %bitcast.57, pred[8,8]{1,0:T(8,128)(4,1)S(1)} %compare_and_fusion), kind=kLoop, calls=%fused_computation.1 | loop fusion | flops 65011712 | bytes 41943104
  208.1 6.5 %copy.29 = bf16[512,256,2,8]{0,1,2,3:T(8,128)(2,1)} copy(bf16[512,256,2,8]{1,0,2,3:T(8,128)(2,1)} %multiply_reduce_fusion) | data formatting | bytes 8388608 | tf_op jit(solution)/shard_map/vrkqc,qrc->vrkc/dot_general | solution.py:42
  214.6 4.6 %all-to-all-start.1 = ((bf16[2,512,8,256]{1,3,0,2:T(8,128)(2,1)}), bf16[2,512,8,256]{1,3,0,2:T(8,128)(2,1)}, u32[]{:S(2)}, u32[]{:S(2)}) async-start(bf16[2,512,8,256]{1,3,0,2:T(8,128)(2,1)} %bitcast.59), calls=%async_computation.1 | async-start | bytes 8388608 | tf_op jit(solution)/shard_map/all_to_all | solution.py:45
  219.1 0.0 reduce-scatter.2.cloned.1.call-start
  219.2 80.0 %psum.7 = bf16[2,512]{1,0:T(2,128)(2,1)S(1)} all-reduce(f32[2,512]{1,0:T(2,128)S(1)} %get-tuple-element.5), channel_id=1, replica_groups=mesh['ka'=8,'band'=4] {'ka'}, use_global_device_ids=true, to_apply=%region_1.0 | all-reduce | flops 1024 | bytes 6144 | tf_op jit(solution)/shard_map/psum | solution.py:31
  299.2 8.2 %all_gather.10 = bf16[2,2048]{1,0:T(2,128)(2,1)S(1)} all-gather(bf16[2,512]{1,0:T(2,128)(2,1)S(1)} %psum.7), channel_id=1, replica_groups=mesh['ka'=8,'band'=4] {'band'}, dimensions={1}, use_global_device_ids=true | all-gather | bytes 10240 | tf_op jit(solution)/shard_map/all_gather | solution.py:32
  307.4 0.0 copy-done
  307.4 0.6 convolution_multiply_fusion
  308.1 5.2 %all-to-all-done.1 = bf16[2,512,8,256]{1,3,0,2:T(8,128)(2,1)} async-done(((bf16[2,512,8,256]{1,3,0,2:T(8,128)(2,1)}), bf16[2,512,8,256]{1,3,0,2:T(8,128)(2,1)}, u32[]{:S(2)}, u32[]{:S(2)}) %all-to-all-start.1) | async-done | bytes 4194336 | tf_op jit(solution)/shard_map/all_to_all | solution.py:45
  313.3 4.5 %copy.18 = bf16[2,512,8,256]{1,3,2,0:T(8,128)(2,1)} copy(bf16[2,512,8,256]{1,3,0,2:T(8,128)(2,1)} %all-to-all-done.1) | data formatting | bytes 8388608 | tf_op jit(solution)/shard_map/all_to_all | solution.py:45
  317.8 0.0 copy-start.4
  317.8 0.0 copy-start.5
  317.8 9.3 %fusion.7 = f32[2,128,896]{1,2,0:T(8,128)} fusion(f32[2,512]{1,0:T(2,128)S(1)} %convolution_multiply_fusion, f32[512,896]{0,1:T(8,128)} %copy.14, bf16[2,512,2048]{1,2,0:T(8,128)(2,1)} %bitcast.60, bf16[1,2048,896]{2,1,0:T(8,128)(2,1)} %all-gather.3.cloned.1.call-done, bf16[1,512,128]{2,1,0:T(8,128)(2,1)S(1)} %copy-done.2), kind=kOutput, calls=%fused_computation.16 | convolution fusion | flops 3995729920 | bytes 10752000 | tf_op jit(solution)/shard_map/ri,vra->via/dot_general | solution.py:53
  327.1 0.0 reduce-scatter.2.cloned.1.call-update
  327.1 0.0 copy-done.4
  327.1 0.0 copy-done.5
  327.1 0.1 broadcast_subtract_fusion
  327.2 39.7 %reduce-scatter.2.cloned.1.call-done = f32[2,128,224]{1,2,0:T(8,128)} async-done(((f32[2,128,896]{1,2,0:T(8,128)}), f32[2,128,224]{1,2,0:T(8,128)}) %reduce-scatter.2.cloned.1.call-update) | async-done | bytes 229392 | tf_op jit(solution)/shard_map/reduce_scatter | solution.py:54
  366.9 1.7 fusion.13
  (4 shorter events, 0.0 us)
Async XLA Ops:
  6.5 300.9 %copy-start = (bf16[512,2048]{1,0:T(8,128)(2,1)S(1)}, bf16[512,2048]{1,0:T(8,128)(2,1)}, u32[]{:S(2)}) copy-start(bf16[512,2048]{1,0:T(8,128)(2,1)} %param.13) | copy-start | bytes 6291460
  6.5 6.1 %copy-start.1 = (f32[1,2,128,224]{2,3,1,0:T(8,128)S(1)}, f32[1,2,128,224]{2,3,1,0:T(8,128)}, u32[]{:S(2)}) copy-start(f32[1,2,128,224]{2,3,1,0:T(8,128)} %param.10) | copy-start | bytes 688132
  6.5 54.8 %all-gather.3.cloned.1.call-start = ((), (), s32[]{:S(2)}) async-start(), calls=%async_computation.4 | async-start | bytes 4587520 | tf_op jit(solution)/shard_map/all_gather | solution.py:17
  7.3 19.0 %copy-start.2 = (bf16[1,512,128]{2,1,0:T(8,128)(2,1)S(1)}, bf16[1,512,128]{2,1,0:T(8,128)(2,1)}, u32[]{:S(2)}) copy-start(bf16[1,512,128]{2,1,0:T(8,128)(2,1)} %param.8) | copy-start | bytes 393220
  70.9 4.7 %copy-start.3 = (s32[8,8]{1,0:T(8,128)S(1)}, s32[8,8]{1,0:T(8,128)}, u32[]{:S(2)}) copy-start(s32[8,8]{1,0:T(8,128)} %param.15) | copy-start | bytes 772
  70.9 98.8 %all-to-all-start = ((bf16[2,512,8,256]{3,1,0,2:T(8,128)(2,1)}), bf16[2,512,8,256]{3,1,0,2:T(8,128)(2,1)}, u32[]{:S(2)}, u32[]{:S(2)}) async-start(bf16[2,512,8,256]{3,1,0,2:T(8,128)(2,1)} %bitcast.58), calls=%async_computation | async-start | bytes 8388608 | tf_op jit(solution)/shard_map/all_to_all | solution.py:38
  214.6 98.7 %all-to-all-start.1 = ((bf16[2,512,8,256]{1,3,0,2:T(8,128)(2,1)}), bf16[2,512,8,256]{1,3,0,2:T(8,128)(2,1)}, u32[]{:S(2)}, u32[]{:S(2)}) async-start(bf16[2,512,8,256]{1,3,0,2:T(8,128)(2,1)} %bitcast.59), calls=%async_computation.1 | async-start | bytes 8388608 | tf_op jit(solution)/shard_map/all_to_all | solution.py:45
  219.1 147.8 %reduce-scatter.2.cloned.1.call-start = ((), (), s32[]{:S(2)}) async-start(), calls=%async_computation.3 | async-start | bytes 1146880 | tf_op jit(solution)/shard_map/reduce_scatter | solution.py:54
  317.8 9.3 %copy-start.4 = (f32[1,224]{1,0:T(1,128)S(1)}, f32[1,224]{1,0:T(1,128)}, u32[]{:S(2)}) copy-start(f32[1,224]{1,0:T(1,128)} %param.12) | copy-start | bytes 2692
  317.8 9.3 %copy-start.5 = (f32[1,128]{1,0:T(1,128)S(1)}, f32[1,128]{1,0:T(1,128)}, u32[]{:S(2)}) copy-start(f32[1,128]{1,0:T(1,128)} %param.11) | copy-start | bytes 1540
Sparse Core Ops, SparseCore 0:
  9.2 52.1 all-gather.2
  327.2 39.6 reduce-scatter.1
where the time goes:
time: 376 us; the launch traced here: 375 us
  waiting for transfers between devices  167 us (44%)
  blocking collectives  102 us (27%)
  local copies, waits for them, and re-layouts  35.4 us (9%)
  other arithmetic  27.7 us (7%)
  matrix products  20.5 us (5%)
  between operations  13.5 us (4%)
  starting transfers between devices  9.34 us (2%)
    all_to_all x1, waiting for transfers between devices, per_device(): lax.all_to_all(split_pairs, 'ka', split_axis=2, concat_axis=2, tiled=True)  89.9 us
    psum x1, blocking collectives, per_device(): density_sum = lax.psum(density_own, 'ka')  80 us
    reduce_scatter x1, waiting for transfers between devices, per_device(): lax.psum_scatter(partial_sums, 'band', scatter_dimension=2, tiled=True)  39.7 us
    all_gather x1, waiting for transfers between devices, per_device(): lax.all_gather(vir_rows[0], 'band', axis=0, tiled=True)  31.7 us
    unnamed x2, other arithmetic  23.3 us
    gather x1, local copies, waits for them, and re-layouts, per_device(): jnp.take(lax.all_to_all(split_pairs, 'ka', split_axis=2, concat_axis=2, t...  14.6 us
    all_gather x1, blocking collectives, per_device(): lax.all_gather(trial_half, 'band', axis=2, tiled=True)  13.6 us
    dot_general x1, matrix products, per_device(): jnp.einsum('ri,vra->via', occ_own, weights, preferred_element_type=jnp.fl...  9.3 us
  transfers between devices with their start and end apart: 4, of which 4 were waited for; matrix products, arithmetic and copies ran while one was open for 4% of the time, Pallas kernels for 0%

commit v1 on v0

v1 whole, which is shorter than its diff:
```python
import functools

import jax
import jax.numpy as jnp
from jax import lax
from jax.experimental import pallas as pl
from jax.experimental.pallas import tpu as pltpu
from jax.sharding import PartitionSpec as P

F32 = jnp.float32
BF16 = jnp.bfloat16
CHUNK = 16


def dot_nt(left, right, **options):
    return lax.dot_general(
        left, right, (((1,), (1,)), ((), ())), preferred_element_type=F32, **options
    )


def kernel(
    kpoints,
    bands,
    vectors,
    occ,
    vir,
    trial,
    coulomb,
    exch,
    table,
    out,
    occ_full,
    occ_tile,
    trial_all,
    half_own,
    half_all,
    dens_all,
    dens_band,
    coulomb_here,
    exch_tile,
    pairs,
    screened,
    sums_send,
    sums_recv,
    sigma_send,
    sigma_recv,
    local_sem,
    occ_band_sem,
    trial_sem,
    occ_point_sem,
    occ_pass_sem,
    half_sem,
    dens_sem,
    dens_band_sem,
    sums_sem,
    sigma_sem,
):
    me = lax.axis_index("ka")
    band = lax.axis_index("band")
    groups = kpoints // 2
    group = lax.div(me, 2)
    core = lax.rem(me, 2)
    sibling = me + 1 - 2 * core
    rows, occupied = occ.shape
    auxiliary = occ_full.shape[0]
    half = rows // 2
    width = auxiliary // groups

    def remote(source, target, sems, slot, device):
        return pltpu.make_async_remote_copy(
            src_ref=source,
            dst_ref=target,
            send_sem=sems.at[0, slot],
            recv_sem=sems.at[1, slot],
            device_id=device,
            device_id_type=pl.DeviceIdType.MESH,
        )

    exch_copy = pltpu.make_async_copy(
        exch.at[
            :,
            pl.ds(pl.multiple_of(core * half, half), half),
            pl.ds(pl.multiple_of(group * width, width), width),
        ],
        exch_tile,
        local_sem.at[0],
    )
    exch_copy.start()
    coulomb_copy = pltpu.make_async_copy(coulomb, coulomb_here, local_sem.at[1])
    coulomb_copy.start()

    barrier = pltpu.get_barrier_semaphore()
    for step in range(1, bands):
        pl.semaphore_signal(
            barrier,
            inc=1,
            device_id=(me, lax.rem(band + step, bands)),
            device_id_type=pl.DeviceIdType.MESH,
        )
    for step in range(1, kpoints):
        pl.semaphore_signal(
            barrier,
            inc=1,
            device_id=(lax.rem(me + step, kpoints), band),
            device_id_type=pl.DeviceIdType.MESH,
        )
    pl.semaphore_wait(barrier, bands + kpoints - 2)

    own_rows = pl.ds(pl.multiple_of(band * rows, rows), rows)
    trial_copies = []
    for step in range(1, bands):
        copy = remote(
            trial, trial_all.at[band], trial_sem, step, (me, lax.rem(band + step, bands))
        )
        copy.start()
        trial_copies.append(copy)
    occ_copies = []
    for step in range(1, bands):
        copy = remote(
            occ, occ_full.at[own_rows], occ_band_sem, step, (me, lax.rem(band + step, bands))
        )
        copy.start()
        occ_copies.append(copy)
    occ_full[own_rows, :] = occ[...]
    trial_all[band] = trial[...]

    for copy in trial_copies:
        copy.wait_recv()
    product = dot_nt(vir[0], trial_all[0])
    for part in range(1, bands):
        product += dot_nt(vir[part], trial_all[part])
    half_own[...] = product.astype(BF16)
    half_all[me] = half_own[pl.ds(pl.multiple_of(core * half, half), half), :]
    half_copies = []
    for step in range(1, kpoints):
        peer = lax.rem(me + step, kpoints)
        peer_core = lax.rem(peer, 2)
        copy = remote(
            half_own.at[pl.ds(pl.multiple_of(peer_core * half, half), half)],
            half_all.at[me],
            half_sem,
            step,
            (peer, band),
        )
        copy.start()
        half_copies.append(copy)

    for copy in occ_copies:
        copy.wait_recv()
    point_copies = []
    for step in range(1, groups):
        peer_group = lax.rem(group + step, groups)
        copy = remote(
            occ_full.at[pl.ds(pl.multiple_of(peer_group * width, width), width)],
            occ_tile.at[me],
            occ_point_sem,
            step,
            (peer_group * 2 + core, band),
        )
        copy.start()
        point_copies.append(copy)
    occ_tile[me] = occ_full[pl.ds(pl.multiple_of(group * width, width), width), :]
    pass_copies = [
        remote(
            occ_full.at[pl.ds(pl.multiple_of(group * width, width), width)],
            occ_tile.at[me],
            occ_pass_sem,
            0,
            (sibling, band),
        )
    ]
    pass_copies[0].start()

    ones = jnp.ones((8, occupied), F32)
    occ_wide = occ[...].astype(F32)
    line = lax.broadcasted_iota(jnp.int32, (8, rows), 0)
    density = jnp.zeros((8, rows), F32)
    for v in range(vectors):
        here = half_own[:, v * occupied : (v + 1) * occupied].astype(F32)
        summed = dot_nt(ones, occ_wide * here, precision=lax.Precision.HIGHEST)
        density = jnp.where(line == v, summed, density)
    dens_all[me] = density
    dens_copies = []
    for step in range(1, kpoints):
        copy = remote(
            dens_all.at[me],
            dens_all.at[me],
            dens_sem,
            step,
            (lax.rem(me + step, kpoints), band),
        )
        copy.start()
        dens_copies.append(copy)

    for step in range(1, groups):
        point_copies[step - 1].wait_recv()
        source = lax.rem(group - step + groups, groups) * 2 + core
        copy = remote(
            occ_tile.at[source], occ_tile.at[source], occ_pass_sem, step, (sibling, band)
        )
        copy.start()
        pass_copies.append(copy)

    for copy in dens_copies:
        copy.wait_recv()
    density = dens_all[0]
    for k in range(1, kpoints):
        density += dens_all[k]
    dens_band[band] = jnp.concatenate([density, jnp.zeros_like(density)], axis=0).astype(BF16)
    dens_band_copies = []
    for step in range(1, bands):
        copy = remote(
            dens_band.at[band],
            dens_band.at[band],
            dens_band_sem,
            step,
            (me, lax.rem(band + step, bands)),
        )
        copy.start()
        dens_band_copies.append(copy)

    for copy in pass_copies:
        copy.wait_recv()
    exch_copy.wait()

    for step in range(kpoints):
        if step:
            half_copies[step - 1].wait_recv()
        source = lax.rem(me - step + kpoints, kpoints)
        for v in range(vectors):
            pairs[source * vectors + v] = dot_nt(
                half_all[source, :, v * occupied : (v + 1) * occupied], occ_tile[source]
            )

    def screen(target):
        sources = [table[target, q] * vectors for q in range(kpoints)]

        def add_rows(chunk, carry):
            here = pl.ds(pl.multiple_of(chunk * CHUNK, CHUNK), CHUNK)
            totals = [jnp.zeros((CHUNK, width), F32) for _ in range(vectors)]
            for q in range(kpoints):
                factor = exch_tile[q, here, :].astype(F32)
                for v in range(vectors):
                    totals[v] += pairs[sources[q] + v, here, :] * factor
            for v in range(vectors):
                screened[v, here, :] = totals[v].astype(BF16)
            return carry

        lax.fori_loop(0, half // CHUNK, add_rows, 0)
        return jnp.concatenate(
            [
                jnp.dot(screened[v], occ_tile[target], preferred_element_type=F32)
                for v in range(vectors)
            ],
            axis=1,
        ).astype(BF16)

    def sums_copy(step):
        target = lax.rem(me + 1 + step, kpoints)
        return remote(
            sums_send.at[target], sums_recv.at[me], sums_sem, step, (target, band)
        )

    def make_sums(step, carry):
        target = lax.rem(me + 1 + step, kpoints)
        sums_send[target] = screen(target)
        sums_copy(step).start()
        return carry

    lax.fori_loop(0, kpoints - 1, make_sums, 0)
    sums_recv[me] = screen(me)

    for copy in dens_band_copies:
        copy.wait_recv()
    coulomb_copy.wait()
    potential = dot_nt(coulomb_here[:, :rows], dens_band[0])
    for part in range(1, bands):
        potential += dot_nt(coulomb_here[:, part * rows : (part + 1) * rows], dens_band[part])
    for step in range(kpoints - 1):
        sums_copy(step).wait_recv()
    pieces = []
    for side in range(2):
        total = sums_recv[side].astype(F32)
        for g in range(1, groups):
            total += sums_recv[2 * g + side].astype(F32)
        lines = slice(side * half, (side + 1) * half)
        direct = [
            2.0 * potential[lines, v : v + 1] * occ_wide[lines] for v in range(vectors)
        ]
        pieces.append(jnp.concatenate(direct, axis=1) - total)
    coupling = jnp.concatenate(pieces, axis=0).T.astype(BF16)

    sigma_copies = []
    for step in range(1, bands):
        peer = lax.rem(band + step, bands)
        sigma_send[step] = jnp.dot(coupling, vir[peer], preferred_element_type=F32).astype(BF16)
        copy = remote(sigma_send.at[step], sigma_recv.at[step], sigma_sem, step, (me, peer))
        copy.start()
        sigma_copies.append(copy)
    result = jnp.dot(coupling, vir[band], preferred_element_type=F32)
    for step in range(1, bands):
        sigma_copies[step - 1].wait_recv()
        result += sigma_recv[step].astype(F32)
    out[...] = result

    for copy in (
        trial_copies
        + occ_copies
        + half_copies
        + point_copies
        + pass_copies
        + dens_copies
        + dens_band_copies
        + sigma_copies
        + [sums_copy(step) for step in range(kpoints - 1)]
    ):
        copy.wait_send()


def coupled_part(kpoints, bands, occ, vir, trial, coulomb, exch, table, vectors):
    rows, occupied = occ.shape
    merged, columns = trial.shape
    auxiliary = coulomb.shape[1]
    half = rows // 2
    width = auxiliary * 2 // kpoints
    vmem = pl.BlockSpec(memory_space=pltpu.VMEM)
    hbm = pl.BlockSpec(memory_space=pl.ANY)
    smem = pl.BlockSpec(memory_space=pltpu.SMEM)
    both = pltpu.SemaphoreType.DMA
    return pl.pallas_call(
        functools.partial(kernel, kpoints, bands, vectors),
        out_shape=jax.ShapeDtypeStruct((merged, columns), F32),
        in_specs=[vmem, vmem, vmem, hbm, hbm, smem],
        out_specs=vmem,
        scratch_shapes=[
            pltpu.VMEM((auxiliary, occupied), BF16),
            pltpu.VMEM((kpoints, width, occupied), BF16),
            pltpu.VMEM((bands, merged, columns), BF16),
            pltpu.VMEM((rows, merged), BF16),
            pltpu.VMEM((kpoints, half, merged), BF16),
            pltpu.VMEM((kpoints, 8, rows), F32),
            pltpu.VMEM((bands, 16, rows), BF16),
            pltpu.VMEM((rows, auxiliary), BF16),
            pltpu.VMEM((kpoints, half, width), BF16),
            pltpu.VMEM((kpoints * vectors, half, width), F32),
            pltpu.VMEM((vectors, half, width), BF16),
            pltpu.VMEM((kpoints, half, merged), BF16),
            pltpu.VMEM((kpoints, half, merged), BF16),
            pltpu.VMEM((bands, merged, columns), BF16),
            pltpu.VMEM((bands, merged, columns), BF16),
            both((2,)),
            both((2, bands)),
            both((2, bands)),
            both((2, kpoints)),
            both((2, kpoints)),
            both((2, kpoints)),
            both((2, kpoints)),
            both((2, bands)),
            both((2, kpoints)),
            both((2, bands)),
        ],
        compiler_params=pltpu.CompilerParams(
            collective_id=0, has_side_effects=True, vmem_limit_bytes=60 * 2**20
        ),
        name="coupled",
    )(occ, vir, trial, coulomb, exch, table)


def per_device(
    occ_rows, vir_rows, trial_vectors, occ_energy, vir_energy, coulomb, exch_kernel, minus_table
):
    kpoints = lax.axis_size("ka")
    bands = lax.axis_size("band")
    _, vectors, occupied, columns = trial_vectors.shape
    rows = occ_rows.shape[1]
    trial_half = trial_vectors[0].astype(BF16).reshape(vectors * occupied, columns)
    vir_parts = vir_rows[0].reshape(rows, bands, columns).transpose(1, 0, 2)
    coupled = coupled_part(
        kpoints,
        bands,
        occ_rows[0],
        vir_parts,
        trial_half,
        coulomb,
        exch_kernel,
        minus_table,
        vectors,
    ).reshape(vectors, occupied, columns)
    energy_gaps = vir_energy[0][None, :] - occ_energy[0][:, None]
    return (energy_gaps[None] * trial_vectors[0] + coupled)[None]


def solution(mesh):
    in_specs = (
        P("ka", "band", None),
        P("ka", "band", None),
        P("ka", None, None, "band"),
        P("ka", None),
        P("ka", "band"),
        P("band", None),
        P(None, "band", None),
        P(),
    )
    out_specs = P("ka", None, None, "band")
    return jax.shard_map(
        per_device, mesh=mesh, in_specs=in_specs, out_specs=out_specs, check_vma=False
    )
```

time: 376 us -> 95.4 us (0.25)
  the two profiles are of different devices: /device:TPU:0 before, /device:TPU:9 now
where the time goes in v1:
time: 95.4 us; the launch traced here: 95.2 us
  Pallas kernels  88.7 us (93%)
  local copies, waits for them, and re-layouts  4.65 us (5%)
  other arithmetic  1.76 us (2%)
    pallas_call x1, Pallas kernels, coupled_part(): pl.pallas_call(functools.partial(kernel, kpoints, bands, vectors), out_sh...  88.7 us

profile of v1, /device:TPU:9, one launch (start us, length us, event | category | flops | bytes accessed | tf_op | source)
XLA Modules:
  0.0 95.2 jit_solution(16910339216652548321)
XLA Ops:
  0.0 0.0 copy-start
  0.0 0.0 copy-start.1
  0.0 0.0 copy-start.2
  0.0 1.5 %copy.11 = bf16[1,512,896]{1,2,0:T(8,128)(2,1)S(1)} copy(bf16[1,512,896]{2,1,0:T(8,128)(2,1)} %param.9) | data formatting | bytes 1835008 | tf_op args[1]
  1.5 1.3 %copy.12 = bf16[512,4,224]{2,0,1:T(8,128)(2,1)} copy(bf16[512,4,224]{0,2,1:T(8,128)(2,1)S(1)} %bitcast.8) | data formatting | bytes 1835008 | tf_op jit(solution)/shard_map/reshape;squeeze | solution.py:377
  2.8 1.0 %convert_element_type.7 = bf16[1,2,128,224]{2,3,1,0:T(8,128)(2,1)S(1)} convert(f32[1,2,128,224]{2,3,1,0:T(8,128)} %param.10) | non-fusion elementwise | flops 57344 | bytes 344064 | tf_op jit(solution)/shard_map/convert_element_type | solution.py:376
  3.8 0.8 copy.13
  4.5 88.7 %coupled.1 = f32[256,224]{1,0:T(8,128)} custom-call(bf16[512,128]{1,0:T(8,128)(2,1)} %bitcast.11, bf16[4,512,224]{2,1,0:T(8,128)(2,1)} %bitcast.7, bf16[256,224]{1,0:T(8,128)(2,1)} %bitcast.10, bf16[512,2048]{1,0:T(8,128)(2,1)} %coulomb.1, bf16[8,512,2048]{2,1,0:T(8,128)(2,1)} %exch.1, s32[8,8]{1,0:T(8,128)} %table.1), custom_call_target="tpu_custom_call" | custom-call | tf_op jit(solution)/shard_map/coupled/pallas_call | solution.py:330
  93.2 1.1 %copy.14 = f32[1,2,128,224]{2,3,1,0:T(8,128)S(1)} copy(f32[1,2,128,224]{3,2,1,0:T(8,128)} %bitcast.9) | data formatting | bytes 458752 | tf_op jit(solution)/shard_map/reshape | solution.py:388
  94.3 0.0 copy-done.1
  94.3 0.0 copy-done.2
  94.3 0.1 broadcast_subtract_fusion
  94.4 0.0 copy-done
  94.5 0.7 multiply_add_fusion
Async XLA Ops:
  0.0 94.4 %copy-start = (f32[1,2,128,224]{2,3,1,0:T(8,128)S(1)}, f32[1,2,128,224]{2,3,1,0:T(8,128)}, u32[]{:S(2)}) copy-start(f32[1,2,128,224]{2,3,1,0:T(8,128)} %param.10) | copy-start | bytes 688132
  0.0 94.3 %copy-start.1 = (f32[1,224]{1,0:T(1,128)S(1)}, f32[1,224]{1,0:T(1,128)}, u32[]{:S(2)}) copy-start(f32[1,224]{1,0:T(1,128)} %param.12) | copy-start | bytes 2692
  0.0 94.3 %copy-start.2 = (f32[1,128]{1,0:T(1,128)S(1)}, f32[1,128]{1,0:T(1,128)}, u32[]{:S(2)}) copy-start(f32[1,128]{1,0:T(1,128)} %param.11) | copy-start | bytes 1540

commit v2 on v1

--- a/solution.py
+++ b/solution.py
@@ -31,7 +31,8 @@
     out,
     occ_full,
     occ_tile,
-    trial_all,
+    trial_full,
+    vir_turned,
     half_own,
     half_all,
     dens_all,
@@ -41,6 +42,7 @@
     pairs,
     screened,
     sums_send,
+    sums_part,
     sums_recv,
     sigma_send,
     sigma_recv,
@@ -52,6 +54,7 @@
     half_sem,
     dens_sem,
     dens_band_sem,
+    part_sem,
     sums_sem,
     sigma_sem,
 ):
@@ -65,12 +68,14 @@
     auxiliary = occ_full.shape[0]
     half = rows // 2
     width = auxiliary // groups
-
-    def remote(source, target, sems, slot, device):
+    columns = trial.shape[1]
+    own_columns = pl.ds(pl.multiple_of(band * columns, columns), columns)
+
+    def remote(source, target, sems, slot, device, send_slot=None):
         return pltpu.make_async_remote_copy(
             src_ref=source,
             dst_ref=target,
-            send_sem=sems.at[0, slot],
+            send_sem=sems.at[0, slot if send_slot is None else send_slot],
             recv_sem=sems.at[1, slot],
             device_id=device,
             device_id_type=pl.DeviceIdType.MESH,
@@ -89,6 +94,8 @@
     coulomb_copy = pltpu.make_async_copy(coulomb, coulomb_here, local_sem.at[1])
     coulomb_copy.start()
 
+    trial_full[:, own_columns, :] = trial[...].astype(BF16)
+
     barrier = pltpu.get_barrier_semaphore()
     for step in range(1, bands):
         pl.semaphore_signal(
@@ -110,7 +117,11 @@
     trial_copies = []
     for step in range(1, bands):
         copy = remote(
-            trial, trial_all.at[band], trial_sem, step, (me, lax.rem(band + step, bands))
+            trial_full.at[:, own_columns],
+            trial_full.at[:, own_columns],
+            trial_sem,
+            step,
+            (me, lax.rem(band + step, bands)),
         )
         copy.start()
         trial_copies.append(copy)
@@ -122,28 +133,45 @@
         copy.start()
         occ_copies.append(copy)
     occ_full[own_rows, :] = occ[...]
-    trial_all[band] = trial[...]
 
     for copy in trial_copies:
         copy.wait_recv()
-    product = dot_nt(vir[0], trial_all[0])
-    for part in range(1, bands):
-        product += dot_nt(vir[part], trial_all[part])
-    half_own[...] = product.astype(BF16)
+    for v in range(vectors):
+        half_own[:, v * occupied : (v + 1) * occupied] = jnp.dot(
+            vir[...], trial_full[v], preferred_element_type=F32
+        ).astype(BF16)
     half_all[me] = half_own[pl.ds(pl.multiple_of(core * half, half), half), :]
-    half_copies = []
-    for step in range(1, kpoints):
-        peer = lax.rem(me + step, kpoints)
-        peer_core = lax.rem(peer, 2)
-        copy = remote(
-            half_own.at[pl.ds(pl.multiple_of(peer_core * half, half), half)],
+    half_rows = [half_own.at[pl.ds(side * half, half)] for side in range(2)]
+    signs = (1, -1)
+    half_copies = [
+        remote(
+            half_own.at[pl.ds(pl.multiple_of((1 - core) * half, half), half)],
             half_all.at[me],
             half_sem,
-            step,
-            (peer, band),
-        )
-        copy.start()
-        half_copies.append(copy)
+            0,
+            (sibling, band),
+        )
+    ]
+    for way, sign in enumerate(signs):
+        next_group = lax.rem(group + sign + groups, groups)
+        for side in range(2):
+            half_copies.append(
+                remote(
+                    half_rows[side],
+                    half_all.at[me],
+                    half_sem,
+                    1 + 2 * way + core,
+                    (next_group * 2 + side, band),
+                    send_slot=1 + 2 * way + side,
+                )
+            )
+    for copy in half_copies[1:] + half_copies[:1]:
+        copy.start()
+
+    def half_arrival(distance, way, owner_core):
+        source = lax.rem(group - signs[way] * distance + groups, groups) * 2 + owner_core
+        slot = (4 * (distance - 1) + 2 * way + owner_core) + 1
+        return source, slot
 
     for copy in occ_copies:
         copy.wait_recv()
@@ -201,36 +229,62 @@
         copy.start()
         pass_copies.append(copy)
 
-    for copy in dens_copies:
-        copy.wait_recv()
-    density = dens_all[0]
-    for k in range(1, kpoints):
-        density += dens_all[k]
-    dens_band[band] = jnp.concatenate([density, jnp.zeros_like(density)], axis=0).astype(BF16)
-    dens_band_copies = []
-    for step in range(1, bands):
-        copy = remote(
-            dens_band.at[band],
-            dens_band.at[band],
-            dens_band_sem,
-            step,
-            (me, lax.rem(band + step, bands)),
-        )
-        copy.start()
-        dens_band_copies.append(copy)
-
-    for copy in pass_copies:
-        copy.wait_recv()
-    exch_copy.wait()
-
-    for step in range(kpoints):
-        if step:
-            half_copies[step - 1].wait_recv()
-        source = lax.rem(me - step + kpoints, kpoints)
+    def make_pairs(source):
         for v in range(vectors):
             pairs[source * vectors + v] = dot_nt(
                 half_all[source, :, v * occupied : (v + 1) * occupied], occ_tile[source]
             )
+
+    arrived = [me, sibling]
+    for distance in range(1, groups // 2 + 1):
+        for way in range(2):
+            for owner_core in range(2):
+                if distance == groups // 2 and owner_core != way:
+                    continue
+                source, slot = half_arrival(distance, way, owner_core)
+                here = half_all.at[source]
+                remote(here, here, half_sem, slot, (sibling, band)).wait_recv()
+                arrived.append(source)
+                farther = distance + 1
+                if farther < groups // 2 or (farther == groups // 2 and owner_core == way):
+                    next_group = lax.rem(group + signs[way] + groups, groups)
+                    copy = remote(
+                        here, here, half_sem, slot + 4, (next_group * 2 + core, band)
+                    )
+                    copy.start()
+                    half_copies.append(copy)
+        if distance == 1:
+            vir_turned[...] = vir[...].T
+            for copy in dens_copies:
+                copy.wait_recv()
+            density = dens_all[0]
+            for k in range(1, kpoints):
+                density += dens_all[k]
+            dens_band[band] = jnp.concatenate(
+                [density, jnp.zeros_like(density)], axis=0
+            ).astype(BF16)
+            dens_band_copies = []
+            for step in range(1, bands):
+                copy = remote(
+                    dens_band.at[band],
+                    dens_band.at[band],
+                    dens_band_sem,
+                    step,
+                    (me, lax.rem(band + step, bands)),
+                )
+                copy.start()
+                dens_band_copies.append(copy)
+            for copy in pass_copies:
+                copy.wait_recv()
+            exch_copy.wait()
+            there = half_all.at[sibling]
+            remote(there, there, half_sem, 0, (sibling, band)).wait_recv()
+            for source in arrived:
+                make_pairs(source)
+        else:
+            for source in arrived:
+                make_pairs(source)
+        arrived = []
 
     def screen(target):
         sources = [table[target, q] * vectors for q in range(kpoints)]
@@ -253,22 +307,61 @@
                 for v in range(vectors)
             ],
             axis=1,
-        ).astype(BF16)
-
-    def sums_copy(step):
-        target = lax.rem(me + 1 + step, kpoints)
-        return remote(
-            sums_send.at[target], sums_recv.at[me], sums_sem, step, (target, band)
-        )
-
-    def make_sums(step, carry):
-        target = lax.rem(me + 1 + step, kpoints)
-        sums_send[target] = screen(target)
-        sums_copy(step).start()
-        return carry
-
-    lax.fori_loop(0, kpoints - 1, make_sums, 0)
-    sums_recv[me] = screen(me)
+        )
+
+    stages = []
+    for distance in range(groups // 2, 0, -1):
+        level = [
+            (distance, way, target_core)
+            for way in range(2)
+            for target_core in range(2)
+            if distance < groups // 2 or target_core == way
+        ]
+        stages += sorted(level, key=lambda stage: stage[1] == stage[2])
+    sums_copies = []
+    for slot, (distance, way, target_core) in enumerate(stages):
+        sign = signs[way]
+        target = lax.rem(group + sign * distance + groups, groups) * 2 + target_core
+        total = screen(target)
+        earlier = (distance + 1, way, target_core)
+        if earlier in stages:
+            before = stages.index(earlier)
+            there = sums_part.at[before]
+            remote(there, there, part_sem, before, (sibling, band)).wait_recv()
+            total += sums_part[before].astype(F32)
+        sums_send[slot] = total.astype(BF16)
+        next_group = lax.rem(group + sign + groups, groups)
+        if distance > 1:
+            copy = remote(
+                sums_send.at[slot],
+                sums_part.at[slot],
+                part_sem,
+                slot,
+                (next_group * 2 + core, band),
+            )
+        else:
+            copy = remote(
+                sums_send.at[slot],
+                sums_recv.at[1 + way, core],
+                sums_sem,
+                2 + 2 * way + core,
+                (next_group * 2 + target_core, band),
+                send_slot=2 + 2 * way + target_core,
+            )
+        copy.start()
+        sums_copies.append(copy)
+    last = len(stages)
+    sums_send[last] = screen(sibling).astype(BF16)
+    copy = remote(
+        sums_send.at[last],
+        sums_recv.at[0, core],
+        sums_sem,
+        0,
+        (sibling, band),
+    )
+    copy.start()
+    sums_copies.append(copy)
+    sums_recv[0, core] = screen(me).astype(BF16)
 
     for copy in dens_band_copies:
         copy.wait_recv()
@@ -276,32 +369,42 @@
     potential = dot_nt(coulomb_here[:, :rows], dens_band[0])
     for part in range(1, bands):
         potential += dot_nt(coulomb_here[:, part * rows : (part + 1) * rows], dens_band[part])
-    for step in range(kpoints - 1):
-        sums_copy(step).wait_recv()
-    pieces = []
-    for side in range(2):
-        total = sums_recv[side].astype(F32)
-        for g in range(1, groups):
-            total += sums_recv[2 * g + side].astype(F32)
-        lines = slice(side * half, (side + 1) * half)
-        direct = [
-            2.0 * potential[lines, v : v + 1] * occ_wide[lines] for v in range(vectors)
-        ]
-        pieces.append(jnp.concatenate(direct, axis=1) - total)
-    coupling = jnp.concatenate(pieces, axis=0).T.astype(BF16)
+    there = sums_recv.at[0, 1 - core]
+    remote(there, there, sums_sem, 0, (sibling, band)).wait_recv()
+    for way in range(2):
+        for side in range(2):
+            there = sums_recv.at[1 + way, side]
+            remote(there, there, sums_sem, 2 + 2 * way + side, (sibling, band)).wait_recv()
+    coupling = []
+    for v in range(vectors):
+        pieces = []
+        for side in range(2):
+            part = slice(v * occupied, (v + 1) * occupied)
+            total = sums_recv[0, side, :, part].astype(F32)
+            for way in range(2):
+                total += sums_recv[1 + way, side, :, part].astype(F32)
+            lines = slice(side * half, (side + 1) * half)
+            pieces.append(2.0 * potential[lines, v : v + 1] * occ_wide[lines] - total)
+        coupling.append(jnp.concatenate(pieces, axis=0).astype(BF16))
+    coupling = jnp.concatenate(coupling, axis=1)
+
+    def sigma_of(peer):
+        peer_columns = pl.ds(pl.multiple_of(peer * columns, columns), columns)
+        return jnp.dot(vir_turned[peer_columns, :], coupling, preferred_element_type=F32)
 
     sigma_copies = []
     for step in range(1, bands):
         peer = lax.rem(band + step, bands)
-        sigma_send[step] = jnp.dot(coupling, vir[peer], preferred_element_type=F32).astype(BF16)
+        sigma_send[step] = sigma_of(peer).astype(BF16)
         copy = remote(sigma_send.at[step], sigma_recv.at[step], sigma_sem, step, (me, peer))
         copy.start()
         sigma_copies.append(copy)
-    result = jnp.dot(coupling, vir[band], preferred_element_type=F32)
+    result = sigma_of(band)
     for step in range(1, bands):
         sigma_copies[step - 1].wait_recv()
         result += sigma_recv[step].astype(F32)
-    out[...] = result
+    for v in range(vectors):
+        out[v] = result[:, v * occupied : (v + 1) * occupied]
 
     for copy in (
         trial_copies
@@ -312,14 +415,15 @@
         + dens_copies
         + dens_band_copies
         + sigma_copies
-        + [sums_copy(step) for step in range(kpoints - 1)]
+        + sums_copies
     ):
         copy.wait_send()
 
 
 def coupled_part(kpoints, bands, occ, vir, trial, coulomb, exch, table, vectors):
     rows, occupied = occ.shape
-    merged, columns = trial.shape
+    columns = trial.shape[1]
+    merged = vectors * occupied
     auxiliary = coulomb.shape[1]
     half = rows // 2
     width = auxiliary * 2 // kpoints
@@ -329,13 +433,14 @@
     both = pltpu.SemaphoreType.DMA
     return pl.pallas_call(
         functools.partial(kernel, kpoints, bands, vectors),
-        out_shape=jax.ShapeDtypeStruct((merged, columns), F32),
+        out_shape=jax.ShapeDtypeStruct(trial.shape, F32),
         in_specs=[vmem, vmem, vmem, hbm, hbm, smem],
         out_specs=vmem,
         scratch_shapes=[
             pltpu.VMEM((auxiliary, occupied), BF16),
             pltpu.VMEM((kpoints, width, occupied), BF16),
-            pltpu.VMEM((bands, merged, columns), BF16),
+            pltpu.VMEM((vectors, bands * columns, occupied), BF16),
+            pltpu.VMEM((bands * columns, rows), BF16),
             pltpu.VMEM((rows, merged), BF16),
             pltpu.VMEM((kpoints, half, merged), BF16),
             pltpu.VMEM((kpoints, 8, rows), F32),
@@ -346,16 +451,18 @@
             pltpu.VMEM((vectors, half, width), BF16),
             pltpu.VMEM((kpoints, half, merged), BF16),
             pltpu.VMEM((kpoints, half, merged), BF16),
-            pltpu.VMEM((bands, merged, columns), BF16),
-            pltpu.VMEM((bands, merged, columns), BF16),
+            pltpu.VMEM((3, 2, half, merged), BF16),
+            pltpu.VMEM((bands, columns, merged), BF16),
+            pltpu.VMEM((bands, columns, merged), BF16),
             both((2,)),
             both((2, bands)),
             both((2, bands)),
             both((2, kpoints)),
             both((2, kpoints)),
-            both((2, kpoints)),
+            both((2, kpoints * 2)),
             both((2, kpoints)),
             both((2, bands)),
+            both((2, kpoints)),
             both((2, kpoints)),
             both((2, bands)),
         ],
@@ -371,23 +478,21 @@
 ):
     kpoints = lax.axis_size("ka")
     bands = lax.axis_size("band")
-    _, vectors, occupied, columns = trial_vectors.shape
-    rows = occ_rows.shape[1]
-    trial_half = trial_vectors[0].astype(BF16).reshape(vectors * occupied, columns)
-    vir_parts = vir_rows[0].reshape(rows, bands, columns).transpose(1, 0, 2)
+    vectors = trial_vectors.shape[1]
+    trial_turned = jnp.swapaxes(trial_vectors[0], 1, 2)
     coupled = coupled_part(
         kpoints,
         bands,
         occ_rows[0],
-        vir_parts,
-        trial_half,
+        vir_rows[0],
+        trial_turned,
         coulomb,
         exch_kernel,
         minus_table,
         vectors,
-    ).reshape(vectors, occupied, columns)
-    energy_gaps = vir_energy[0][None, :] - occ_energy[0][:, None]
-    return (energy_gaps[None] * trial_vectors[0] + coupled)[None]
+    )
+    energy_gaps = vir_energy[0][:, None] - occ_energy[0][None, :]
+    return jnp.swapaxes(energy_gaps[None] * trial_turned + coupled, 1, 2)[None]
 
 
 def solution(mesh):

time: 95.4 us -> 77.5 us (0.81)
  the two profiles are of different devices: /device:TPU:9 before, /device:TPU:0 now
where the time goes in v2:
time: 77.5 us; the launch traced here: 77.4 us
  Pallas kernels  74.9 us (97%)
  other arithmetic  2.48 us (3%)
    pallas_call x1, Pallas kernels, coupled_part(): pl.pallas_call(functools.partial(kernel, kpoints, bands, vectors), out_sh...  74.9 us
    broadcast_in_dim x1, other arithmetic, per_device(): return jnp.swapaxes(energy_gaps[None] * trial_turned + coupled, 1, 2)[None]  1.66 us

profile of v2, /device:TPU:0, one launch (start us, length us, event | category | flops | bytes accessed | tf_op | source)
XLA Modules:
  0.0 77.4 jit_solution(17953276823054041405)
XLA Ops:
  0.0 0.0 copy-start
  0.0 0.8 %broadcast_subtract_fusion = f32[224,128]{1,0:T(8,128)S(1)} fusion(f32[128]{0:T(128)} %bitcast.16, f32[224]{0:T(256)} %bitcast.15), kind=kLoop, calls=%fused_computation.1 | loop fusion | flops 28672 | bytes 116096 | tf_op jit(solution)/shard_map/sub | solution.py:494
  0.8 74.9 %coupled.1 = f32[2,224,128]{2,1,0:T(8,128)} custom-call(bf16[512,128]{1,0:T(8,128)(2,1)} %bitcast.14, bf16[512,896]{1,0:T(8,128)(2,1)} %bitcast.13, f32[2,224,128]{2,1,0:T(8,128)} %bitcast.12, bf16[512,2048]{1,0:T(8,128)(2,1)} %coulomb.1, bf16[8,512,2048]{2,1,0:T(8,128)(2,1)} %exch.1, s32[8,8]{1,0:T(8,128)} %table.1), custom_call_target="tpu_custom_call" | custom-call | tf_op jit(solution)/shard_map/coupled/pallas_call | solution.py:434
  75.7 0.0 copy-done
  75.7 1.7 %add_bitcast_fusion = f32[1,2,128,224]{2,3,1,0:T(8,128)} fusion(f32[2,224,128]{2,1,0:T(8,128)} %coupled.1, f32[224,128]{1,0:T(8,128)S(1)} %broadcast_subtract_fusion, f32[1,2,128,224]{2,3,1,0:T(8,128)S(1)} %copy-done), kind=kLoop, calls=%fused_computation | loop fusion | flops 114688 | bytes 802816 | tf_op jit(solution)/shard_map/broadcast_in_dim | solution.py:495
Async XLA Ops:
  0.0 75.7 %copy-start = (f32[1,2,128,224]{2,3,1,0:T(8,128)S(1)}, f32[1,2,128,224]{2,3,1,0:T(8,128)}, u32[]{:S(2)}) copy-start(f32[1,2,128,224]{2,3,1,0:T(8,128)} %param.10) | copy-start | bytes 688132

commit v3 on v2

--- a/solution.py
+++ b/solution.py
@@ -69,6 +69,12 @@
     half = rows // 2
     width = auxiliary // groups
     columns = trial.shape[1]
+    piece = rows // groups
+    scattered = piece % 128 == 0
+
+    def tile_of(k):
+        return lax.rem(k, 2) * groups + lax.div(k, 2)
+
     own_columns = pl.ds(pl.multiple_of(band * columns, columns), columns)
 
     def remote(source, target, sems, slot, device, send_slot=None):
@@ -81,17 +87,23 @@
             device_id_type=pl.DeviceIdType.MESH,
         )
 
-    exch_copy = pltpu.make_async_copy(
-        exch.at[
-            :,
-            pl.ds(pl.multiple_of(core * half, half), half),
-            pl.ds(pl.multiple_of(group * width, width), width),
-        ],
-        exch_tile,
-        local_sem.at[0],
-    )
-    exch_copy.start()
-    coulomb_copy = pltpu.make_async_copy(coulomb, coulomb_here, local_sem.at[1])
+    blocks = bands if scattered else 1
+    block = width // blocks
+    exch_copies = []
+    for part in range(blocks):
+        first = part * rows + group * piece if scattered else group * width
+        copy = pltpu.make_async_copy(
+            exch.at[
+                :,
+                pl.ds(pl.multiple_of(core * half, half), half),
+                pl.ds(pl.multiple_of(first, 128), block),
+            ],
+            exch_tile.at[:, :, pl.ds(part * block, block)],
+            local_sem.at[1 + part],
+        )
+        copy.start()
+        exch_copies.append(copy)
+    coulomb_copy = pltpu.make_async_copy(coulomb, coulomb_here, local_sem.at[0])
     coulomb_copy.start()
 
     trial_full[:, own_columns, :] = trial[...].astype(BF16)
@@ -126,13 +138,45 @@
         copy.start()
         trial_copies.append(copy)
     occ_copies = []
-    for step in range(1, bands):
-        copy = remote(
-            occ, occ_full.at[own_rows], occ_band_sem, step, (me, lax.rem(band + step, bands))
-        )
-        copy.start()
-        occ_copies.append(copy)
-    occ_full[own_rows, :] = occ[...]
+    point_copies = []
+    own_piece = pl.ds(pl.multiple_of(band * piece, piece), piece)
+    mine = tile_of(me)
+    if scattered:
+        for step in range(1, groups):
+            peer_group = lax.rem(group + step, groups)
+            copy = remote(
+                occ.at[pl.ds(pl.multiple_of(peer_group * piece, piece), piece)],
+                occ_tile.at[mine, own_piece],
+                occ_point_sem,
+                step,
+                (peer_group * 2 + core, band),
+            )
+            copy.start()
+            point_copies.append(copy)
+        occ_tile[mine, own_piece, :] = occ[
+            pl.ds(pl.multiple_of(group * piece, piece), piece), :
+        ]
+        for copy in point_copies:
+            copy.wait_recv()
+        own_tiles = pl.ds(core * groups, groups)
+        for step in range(1, bands):
+            copy = remote(
+                occ_tile.at[own_tiles, own_piece],
+                occ_tile.at[own_tiles, own_piece],
+                occ_band_sem,
+                step,
+                (me, lax.rem(band + step, bands)),
+            )
+            copy.start()
+            occ_copies.append(copy)
+    else:
+        for step in range(1, bands):
+            copy = remote(
+                occ, occ_full.at[own_rows], occ_band_sem, step, (me, lax.rem(band + step, bands))
+            )
+            copy.start()
+            occ_copies.append(copy)
+        occ_full[own_rows, :] = occ[...]
 
     for copy in trial_copies:
         copy.wait_recv()
@@ -172,32 +216,6 @@
         source = lax.rem(group - signs[way] * distance + groups, groups) * 2 + owner_core
         slot = (4 * (distance - 1) + 2 * way + owner_core) + 1
         return source, slot
-
-    for copy in occ_copies:
-        copy.wait_recv()
-    point_copies = []
-    for step in range(1, groups):
-        peer_group = lax.rem(group + step, groups)
-        copy = remote(
-            occ_full.at[pl.ds(pl.multiple_of(peer_group * width, width), width)],
-            occ_tile.at[me],
-            occ_point_sem,
-            step,
-            (peer_group * 2 + core, band),
-        )
-        copy.start()
-        point_copies.append(copy)
-    occ_tile[me] = occ_full[pl.ds(pl.multiple_of(group * width, width), width), :]
-    pass_copies = [
-        remote(
-            occ_full.at[pl.ds(pl.multiple_of(group * width, width), width)],
-            occ_tile.at[me],
-            occ_pass_sem,
-            0,
-            (sibling, band),
-        )
-    ]
-    pass_copies[0].start()
 
     ones = jnp.ones((8, occupied), F32)
     occ_wide = occ[...].astype(F32)
@@ -220,11 +238,49 @@
         copy.start()
         dens_copies.append(copy)
 
-    for step in range(1, groups):
+    for copy in occ_copies:
+        copy.wait_recv()
+    if scattered:
+        pass_copies = [
+            remote(
+                occ_tile.at[own_tiles],
+                occ_tile.at[own_tiles],
+                occ_pass_sem,
+                0,
+                (sibling, band),
+            )
+        ]
+        pass_copies[0].start()
+    else:
+        for step in range(1, groups):
+            peer_group = lax.rem(group + step, groups)
+            copy = remote(
+                occ_full.at[pl.ds(pl.multiple_of(peer_group * width, width), width)],
+                occ_tile.at[mine],
+                occ_point_sem,
+                step,
+                (peer_group * 2 + core, band),
+            )
+            copy.start()
+            point_copies.append(copy)
+        occ_tile[mine] = occ_full[pl.ds(pl.multiple_of(group * width, width), width), :]
+        pass_copies = [
+            remote(
+                occ_full.at[pl.ds(pl.multiple_of(group * width, width), width)],
+                occ_tile.at[mine],
+                occ_pass_sem,
+                0,
+                (sibling, band),
+            )
+        ]
+        pass_copies[0].start()
+
+
+    for step in range(1, 1 if scattered else groups):
         point_copies[step - 1].wait_recv()
         source = lax.rem(group - step + groups, groups) * 2 + core
         copy = remote(
-            occ_tile.at[source], occ_tile.at[source], occ_pass_sem, step, (sibling, band)
+            occ_tile.at[tile_of(source)], occ_tile.at[tile_of(source)], occ_pass_sem, step, (sibling, band)
         )
         copy.start()
         pass_copies.append(copy)
@@ -232,7 +288,7 @@
     def make_pairs(source):
         for v in range(vectors):
             pairs[source * vectors + v] = dot_nt(
-                half_all[source, :, v * occupied : (v + 1) * occupied], occ_tile[source]
+                half_all[source, :, v * occupied : (v + 1) * occupied], occ_tile[tile_of(source)]
             )
 
     arrived = [me, sibling]
@@ -276,7 +332,8 @@
                 dens_band_copies.append(copy)
             for copy in pass_copies:
                 copy.wait_recv()
-            exch_copy.wait()
+            for copy in exch_copies:
+                copy.wait()
             there = half_all.at[sibling]
             remote(there, there, half_sem, 0, (sibling, band)).wait_recv()
             for source in arrived:
@@ -303,7 +360,7 @@
         lax.fori_loop(0, half // CHUNK, add_rows, 0)
         return jnp.concatenate(
             [
-                jnp.dot(screened[v], occ_tile[target], preferred_element_type=F32)
+                jnp.dot(screened[v], occ_tile[tile_of(target)], preferred_element_type=F32)
                 for v in range(vectors)
             ],
             axis=1,
@@ -454,7 +511,7 @@
             pltpu.VMEM((3, 2, half, merged), BF16),
             pltpu.VMEM((bands, columns, merged), BF16),
             pltpu.VMEM((bands, columns, merged), BF16),
-            both((2,)),
+            both((1 + bands,)),
             both((2, bands)),
             both((2, bands)),
             both((2, kpoints)),

time: 77.5 us -> 67.3 us (0.87)
  Pallas kernels: 74.9 us -> 64.6 us
    pallas_call x1, Pallas kernels: 74.9 us -> 64.6 us  [coupled_part(): pl.pallas_call(functools.partial(kernel, kpoints, bands, vectors), out_sh...]
where the time goes in v3:
time: 67.3 us; the launch traced here: 67.1 us
  Pallas kernels  64.6 us (96%)
  other arithmetic  2.48 us (4%)
    pallas_call x1, Pallas kernels, coupled_part(): pl.pallas_call(functools.partial(kernel, kpoints, bands, vectors), out_sh...  64.6 us
    broadcast_in_dim x1, other arithmetic, per_device(): return jnp.swapaxes(energy_gaps[None] * trial_turned + coupled, 1, 2)[None]  1.66 us

profile of v3, /device:TPU:0, one launch (start us, length us, event | category | flops | bytes accessed | tf_op | source)
XLA Modules:
  0.0 67.1 jit_solution(1218864177674911831)
XLA Ops:
  0.0 0.0 copy-start
  0.0 0.8 %broadcast_subtract_fusion = f32[224,128]{1,0:T(8,128)S(1)} fusion(f32[128]{0:T(128)} %bitcast.16, f32[224]{0:T(256)} %bitcast.15), kind=kLoop, calls=%fused_computation.1 | loop fusion | flops 28672 | bytes 116096 | tf_op jit(solution)/shard_map/sub | solution.py:551
  0.8 64.6 %coupled.1 = f32[2,224,128]{2,1,0:T(8,128)} custom-call(bf16[512,128]{1,0:T(8,128)(2,1)} %bitcast.14, bf16[512,896]{1,0:T(8,128)(2,1)} %bitcast.13, f32[2,224,128]{2,1,0:T(8,128)} %bitcast.12, bf16[512,2048]{1,0:T(8,128)(2,1)} %coulomb.1, bf16[8,512,2048]{2,1,0:T(8,128)(2,1)} %exch.1, s32[8,8]{1,0:T(8,128)} %table.1), custom_call_target="tpu_custom_call" | custom-call | tf_op jit(solution)/shard_map/coupled/pallas_call | solution.py:491
  65.5 0.0 copy-done
  65.5 1.7 %add_bitcast_fusion = f32[1,2,128,224]{2,3,1,0:T(8,128)} fusion(f32[2,224,128]{2,1,0:T(8,128)} %coupled.1, f32[224,128]{1,0:T(8,128)S(1)} %broadcast_subtract_fusion, f32[1,2,128,224]{2,3,1,0:T(8,128)S(1)} %copy-done), kind=kLoop, calls=%fused_computation | loop fusion | flops 114688 | bytes 802816 | tf_op jit(solution)/shard_map/broadcast_in_dim | solution.py:552
Async XLA Ops:
  0.0 65.5 %copy-start = (f32[1,2,128,224]{2,3,1,0:T(8,128)S(1)}, f32[1,2,128,224]{2,3,1,0:T(8,128)}, u32[]{:S(2)}) copy-start(f32[1,2,128,224]{2,3,1,0:T(8,128)} %param.10) | copy-start | bytes 688132
